TPU v7x, 32 devices: a whole 2x2x4 slice. The times are simulated.
32 devices in a mesh: row: 4 (over z), col: 4 (over y, x), layer: 2 (over core).
Axes of the slice: x: 2, y: 2, z: 4, core: 2. Of those that a mesh axis runs over, the one named last changes fastest.
Arguments:
- wavefunction: float32 [4096, 4096], P('row', 'col'), may hold values from -0.015625 to 1.515625
- start_block: float32 [4096, 2048], P(('col', 'layer'), 'row'), may hold values from -6 to 6
Outputs:
- basis: float32 [4096, 2048], P(('col', 'layer'), 'row')
All inputs are finite; a program needn't handle non-finite values.
Results may differ from a plain program's by a relative error of at most 0.0003.
Values sent between devices are 32-bit elements; how exact they have to be, the bound alone decides.
No kernel may reach another device: no remote copies, remote signals or barrier semaphores. Data moves between devices by JAX's collectives and lax.ppermute only.
A program may use at most 128 MiB of HBM per device.

v0:
```python
import math
import jax
import jax.numpy as jnp
from jax import lax
from jax.sharding import PartitionSpec as P


def spread(x, axis, root):
    mine = lax.axis_index(axis) == root
    return lax.psum(jnp.where(mine, x, jnp.zeros_like(x)), axis)


def cross(left, right):
    return lax.dot_general(
        left,
        right,
        (((0,), (0,)), ((), ())),
        precision=lax.Precision.HIGHEST,
        preferred_element_type=jnp.float32,
    )


def times(left, right):
    return jnp.dot(left, right, precision=lax.Precision.HIGHEST, preferred_element_type=jnp.float32)


def apply_density(rho_slab, basis_block):
    return lax.psum_scatter(
        cross(rho_slab, basis_block), ("col", "layer"), scatter_dimension=0, tiled=True
    )


def orthonormalize(image_block):
    panel_owner = lax.axis_index("row")
    panels = lax.axis_size("row")
    current = image_block
    gram_matrix = lax.psum(cross(current, current), ("col", "layer"))
    for panel_index in range(panels):
        factor = jnp.linalg.cholesky(gram_matrix)
        new_basis = jax.scipy.linalg.solve_triangular(factor, current.T, lower=True).T
        current = jnp.where(panel_owner == panel_index, new_basis, current)
        if panel_index + 1 < panels:
            chosen = spread(current, "row", panel_index)
            later = panel_owner > panel_index
            correlation, square = lax.psum(
                (cross(chosen, current), cross(current, current)), ("col", "layer")
            )
            current = jnp.where(later, current - times(chosen, correlation), current)
            gram_matrix = jnp.where(later, square - cross(correlation, correlation), square)
    return current


def shards(wavefunction, start_block):
    layers = lax.axis_size("layer")
    column_width = wavefunction.shape[1] // layers
    own_slice = lax.dynamic_slice_in_dim(
        wavefunction, lax.axis_index("layer") * column_width, column_width, 1
    )
    own_rows = lax.all_gather(own_slice, "col", axis=1, tiled=True)
    partner = spread(own_rows, "row", lax.axis_index("col"))
    rho_part = lax.psum_scatter(
        lax.dot_general(
            partner,
            own_rows,
            (((1,), (1,)), ((), ())),
            precision=lax.Precision.HIGHEST,
            preferred_element_type=jnp.float32,
        ),
        "layer",
        scatter_dimension=0,
        tiled=True,
    )
    rho_slab = lax.all_gather(rho_part, "row", axis=1, tiled=True)
    current = start_block
    image_block = apply_density(rho_slab, current)
    current = orthonormalize(image_block)
    return current * math.sqrt(rho_slab.shape[1])


def solution(mesh):
    placed = (P("row", "col"), P(("col", "layer"), "row"))
    return jax.shard_map(
        shards, mesh=mesh, in_specs=placed, out_specs=P(("col", "layer"), "row"), check_vma=False
    )
```

profile of v0, /device:TPU:0, one launch (start us, length us, event | category | flops | bytes accessed | tf_op | source)
XLA Modules:
  0.0 1721.6 jit_solution(5460350467099761118)
XLA Ops:
  9.9 90.3 %all-gather.3.cloned.1.call-done = f32[1024,2048]{1,0:T(8,128)} async-done(((f32[1024,512]{1,0:T(8,128)}), f32[1024,2048]{1,0:T(8,128)}) %all-gather.3.cloned.1.call-update) | async-done | bytes 8388624 | tf_op jit(solution)/shard_map/all_gather | solution.py:59
  108.5 290.9 %all-reduce.13.cloned.1.call-done = f32[1024,2048]{1,0:T(8,128)} async-done(((f32[1024,2048]{1,0:T(8,128)}), f32[1024,2048]{1,0:T(8,128)}) %all-reduce.13.cloned.1.call-update) | async-done | bytes 8388624 | tf_op jit(solution)/shard_map/psum | solution.py:10
  399.4 32.1 %fusion.156 = f32[1024,1024]{1,0:T(8,128)} fusion(f32[1024,2048]{1,0:T(8,128)} %all-reduce.13.cloned.1.call-done, f32[1024,2048]{1,0:T(8,128)} %all-gather.3.cloned.1.call-done), kind=kOutput, calls=%fused_computation.284 | convolution fusion | flops 25769803776 | bytes 20971520 | tf_op jit(solution)/shard_map/dot_general | solution.py:62
  443.1 152.0 %all-gather.5.cloned.1.call-done = f32[512,4096]{1,0:T(8,128)} async-done(((f32[512,1024]{1,0:T(8,128)}), f32[512,4096]{1,0:T(8,128)}) %all-gather.5.cloned.1.call-update) | async-done | bytes 8388624 | tf_op jit(solution)/shard_map/all_gather | solution.py:73
  595.1 17.1 fusion.157
  612.2 69.6 %reduce-scatter.5.cloned.1.call-done = f32[512,512]{0,1:T(8,128)} async-done(((f32[4096,512]{0,1:T(8,128)}), f32[512,512]{0,1:T(8,128)}) %reduce-scatter.5.cloned.1.call-update) | async-done | bytes 1048592 | tf_op jit(solution)/shard_map/reduce_scatter | solution.py:28
  686.9 56.3 %all-reduce.15.cloned.1.call-done = f32[512,512]{0,1:T(8,128)} async-done(((f32[512,512]{0,1:T(8,128)}), f32[512,512]{0,1:T(8,128)}) %all-reduce.15.cloned.1.call-update) | async-done | bytes 1048592 | tf_op jit(solution)/shard_map/psum | solution.py:37
  813.8 11.7 cholesky.519
  838.3 39.3 %custom-call.38 = f32[4,128,128]{1,2,0:T(8,128)S(1)} custom-call(f32[4,128,128]{2,1,0:T(8,128)S(1)} %get-tuple-element.33), custom_call_target="InvertDiagBlocksLowerTriangular" | custom-call | tf_op jit(solution)/shard_map/jit(_solve_triangular)/triangular_solve | solution.py:40
  884.9 48.4 %all-reduce.17.cloned.1.call-done = f32[512,512]{0,1:T(8,128)} async-done(((f32[512,512]{0,1:T(8,128)}), f32[512,512]{0,1:T(8,128)}) %all-reduce.17.cloned.1.call-update) | async-done | bytes 1048592 | tf_op jit(solution)/shard_map/psum | solution.py:10
  937.8 60.8 %all-reduce.27.cloned.1.call-done = (f32[512,512]{1,0:T(8,128)}, f32[512,512]{0,1:T(8,128)}) async-done(((f32[512,512]{1,0:T(8,128)}, f32[512,512]{0,1:T(8,128)}), (f32[512,512]{1,0:T(8,128)}, f32[512,512]{0,1:T(8,128)})) %all-reduce.27.cloned.1.call-update) | async-done | bytes 2097168 | tf_op jit(solution)/shard_map/psum | solution.py:45
  1030.6 11.9 cholesky.553
  1078.8 12.1 cholesky.591
  1106.6 39.3 %custom-call.42 = f32[4,128,128]{1,2,0:T(8,128)S(1)} custom-call(f32[4,128,128]{2,1,0:T(8,128)S(1)} %get-tuple-element.34), custom_call_target="InvertDiagBlocksLowerTriangular" | custom-call | tf_op jit(solution)/shard_map/jit(_solve_triangular)/triangular_solve | solution.py:40
  1159.0 48.2 %all-reduce.19.cloned.1.call-done = f32[512,512]{0,1:T(8,128)} async-done(((f32[512,512]{0,1:T(8,128)}), f32[512,512]{0,1:T(8,128)}) %all-reduce.19.cloned.1.call-update) | async-done | bytes 1048592 | tf_op jit(solution)/shard_map/psum | solution.py:10
  1211.5 61.1 %all-reduce.25.cloned.1.call-done = (f32[512,512]{1,0:T(8,128)}, f32[512,512]{0,1:T(8,128)}) async-done(((f32[512,512]{1,0:T(8,128)}, f32[512,512]{0,1:T(8,128)}), (f32[512,512]{1,0:T(8,128)}, f32[512,512]{0,1:T(8,128)})) %all-reduce.25.cloned.1.call-update) | async-done | bytes 2097168 | tf_op jit(solution)/shard_map/psum | solution.py:45
  1304.5 11.9 cholesky.625
  1352.8 12.1 cholesky.663
  1380.5 39.3 %custom-call.46 = f32[4,128,128]{1,2,0:T(8,128)S(1)} custom-call(f32[4,128,128]{2,1,0:T(8,128)S(1)} %get-tuple-element.35), custom_call_target="InvertDiagBlocksLowerTriangular" | custom-call | tf_op jit(solution)/shard_map/jit(_solve_triangular)/triangular_solve | solution.py:40
  1433.1 48.0 %all-reduce.21.cloned.1.call-done = f32[512,512]{0,1:T(8,128)} async-done(((f32[512,512]{0,1:T(8,128)}), f32[512,512]{0,1:T(8,128)}) %all-reduce.21.cloned.1.call-update) | async-done | bytes 1048592 | tf_op jit(solution)/shard_map/psum | solution.py:10
  1485.2 61.3 %all-reduce.23.cloned.1.call-done = (f32[512,512]{1,0:T(8,128)}, f32[512,512]{0,1:T(8,128)}) async-done(((f32[512,512]{1,0:T(8,128)}, f32[512,512]{0,1:T(8,128)}), (f32[512,512]{1,0:T(8,128)}, f32[512,512]{0,1:T(8,128)})) %all-reduce.23.cloned.1.call-update) | async-done | bytes 2097168 | tf_op jit(solution)/shard_map/psum | solution.py:45
  1631.5 11.7 cholesky.735
  1650.2 13.7 while.11
  1663.9 40.1 %custom-call.50 = f32[4,128,128]{1,2,0:T(8,128)S(1)} custom-call(f32[4,128,128]{2,1,0:T(8,128)} %get-tuple-element.36), custom_call_target="InvertDiagBlocksLowerTriangular" | custom-call | tf_op jit(solution)/shard_map/jit(_solve_triangular)/triangular_solve | solution.py:40
  (253 shorter events, 462.2 us)
Async XLA Ops:
  6.5 588.5 %copy-start = (f32[512,512]{1,0:T(8,128)S(1)}, f32[512,512]{1,0:T(8,128)}, u32[]{:S(2)}) copy-start(f32[512,512]{1,0:T(8,128)} %param.6) | copy-start | bytes 3145732
  6.5 93.6 %all-gather.3.cloned.1.call-start = ((), (), s32[]{:S(2)}) async-start(), calls=%async_computation.2 | async-start | bytes 10485760 | tf_op jit(solution)/shard_map/all_gather | solution.py:59
  9.8 389.6 %all-reduce.13.cloned.1.call-start = ((), (), s32[]{:S(2)}) async-start(), calls=%async_computation.3 | async-start | bytes 16777216 | tf_op jit(solution)/shard_map/psum | solution.py:10
  108.4 334.3 %reduce-scatter.3.cloned.1.call-start = ((), (), s32[]{:S(2)}) async-start(), calls=%async_computation.4 | async-start | bytes 6291456 | tf_op jit(solution)/shard_map/reduce_scatter | solution.py:61
  431.5 163.5 %all-gather.5.cloned.1.call-start = ((), (), s32[]{:S(2)}) async-start(), calls=%async_computation.5 | async-start | bytes 10485760 | tf_op jit(solution)/shard_map/all_gather | solution.py:73
  442.7 239.1 %reduce-scatter.5.cloned.1.call-start = ((), (), s32[]{:S(2)}) async-start(), calls=%async_computation.6 | async-start | bytes 9437184 | tf_op jit(solution)/shard_map/reduce_scatter | solution.py:28
  612.2 131.0 %all-reduce.15.cloned.1.call-start = ((), (), s32[]{:S(2)}) async-start(), calls=%async_computation.7 | async-start | bytes 2097152 | tf_op jit(solution)/shard_map/psum | solution.py:37
  681.8 195.8 %copy-start.2 = (f32[512,512]{0,1:T(8,128)S(1)}, f32[512,512]{0,1:T(8,128)}, u32[]{:S(2)}) copy-start(f32[512,512]{0,1:T(8,128)} %reduce-scatter.5.cloned.1.call-done) | copy-start | bytes 3145732
  686.3 247.0 %all-reduce.17.cloned.1.call-start = ((), (), s32[]{:S(2)}) async-start(), calls=%async_computation.8 | async-start | bytes 2097152 | tf_op jit(solution)/shard_map/psum | solution.py:10
  882.0 116.7 %all-reduce.27.cloned.1.call-start = ((), (), s32[]{:S(2)}) async-start(), calls=%async_computation.13 | async-start | bytes 4194304 | tf_op jit(solution)/shard_map/psum | solution.py:45
  937.4 269.8 %all-reduce.19.cloned.1.call-start = ((), (), s32[]{:S(2)}) async-start(), calls=%async_computation.9 | async-start | bytes 2097152 | tf_op jit(solution)/shard_map/psum | solution.py:10
  998.7 147.3 %copy-start.4 = (f32[512,512]{1,0:T(8,128)S(1)}, f32[512,512]{1,0:T(8,128)}, u32[]{:S(2)}) copy-start(f32[512,512]{1,0:T(8,128)} %get-tuple-element.73) | copy-start | bytes 3145732
  1005.4 1.0 copy-start.6
  1156.1 116.5 %all-reduce.25.cloned.1.call-start = ((), (), s32[]{:S(2)}) async-start(), calls=%async_computation.12 | async-start | bytes 4194304 | tf_op jit(solution)/shard_map/psum | solution.py:45
  1211.3 269.9 %all-reduce.21.cloned.1.call-start = ((), (), s32[]{:S(2)}) async-start(), calls=%async_computation.10 | async-start | bytes 2097152 | tf_op jit(solution)/shard_map/psum | solution.py:10
  1272.6 147.3 %copy-start.5 = (f32[512,512]{1,0:T(8,128)S(1)}, f32[512,512]{1,0:T(8,128)}, u32[]{:S(2)}) copy-start(f32[512,512]{1,0:T(8,128)} %get-tuple-element.71) | copy-start | bytes 3145732
  1279.3 1.0 copy-start.7
  1430.1 116.5 %all-reduce.23.cloned.1.call-start = ((), (), s32[]{:S(2)}) async-start(), calls=%async_computation.11 | async-start | bytes 4194304 | tf_op jit(solution)/shard_map/psum | solution.py:45
  1546.5 157.5 %copy-start.3 = (f32[512,512]{1,0:T(8,128)S(1)}, f32[512,512]{1,0:T(8,128)}, u32[]{:S(2)}) copy-start(f32[512,512]{1,0:T(8,128)} %get-tuple-element.69) | copy-start | bytes 3145732
  1553.2 1.0 copy-start.8
  1647.0 67.5 %copy-start.1 = (f32[512,512]{1,0:T(8,128)S(1)}, f32[512,512]{1,0:T(8,128)}, u32[]{:S(2)}) copy-start(f32[512,512]{1,0:T(8,128)} %param.6) | copy-start | bytes 3145732
Sparse Core Ops, SparseCore 0:
  9.9 90.1 all-gather.2
  108.5 290.8 all-reduce.12
  431.7 10.9 reduce-scatter.2
  444.1 150.8 all-gather.4
  612.3 69.4 reduce-scatter.4
  686.4 56.6 all-reduce.14
  882.1 51.1 all-reduce.16
  937.5 61.1 all-reduce.26
  1156.2 50.9 all-reduce.18
  1211.4 61.1 all-reduce.24
  1430.2 50.9 all-reduce.20
  1485.3 61.1 all-reduce.22
where the time goes:
time: 1730 us; the launch traced here: 1720 us
  waiting for transfers between devices  998 us (58%)
  other arithmetic  500 us (29%)
  matrix products  136 us (8%)
  local copies, waits for them, and re-layouts  59.8 us (3%)
  between operations  24.6 us (1%)
    psum x4, waiting for transfers between devices, spread(): return lax.psum(jnp.where(mine, x, jnp.zeros_like(x)), axis)  436 us
    another operation x59, other arithmetic, orthonormalize(): factor = jnp.linalg.cholesky(gram_matrix)  319 us
    psum x3, waiting for transfers between devices, orthonormalize(): lax.psum((cross(chosen, current), cross(current, current)), ('col', 'laye...  183 us
    another operation x9, other arithmetic, orthonormalize(): jax.scipy.linalg.solve_triangular(factor, current.T, lower=True)  163 us
    all_gather x1, waiting for transfers between devices, shards(): rho_slab = lax.all_gather(rho_part, 'row', axis=1, tiled=True)  152 us
    all_gather x1, waiting for transfers between devices, shards(): own_rows = lax.all_gather(own_slice, 'col', axis=1, tiled=True)  90.3 us
    reduce_scatter x1, waiting for transfers between devices, apply_density(): lax.psum_scatter(cross(rho_slab, basis_block), ('col', 'layer'), scatter_...  69.6 us
    psum x1, waiting for transfers between devices, orthonormalize(): gram_matrix = lax.psum(cross(current, current), ('col', 'layer'))  56.3 us
  transfers between devices with their start and end apart: 12, of which 12 were waited for; matrix products, arithmetic and copies ran while one was open for 0% of the time, Pallas kernels for 0%

commit v1 on v0

--- a/solution.py
+++ b/solution.py
@@ -43,7 +43,7 @@
             chosen = spread(current, "row", panel_index)
             later = panel_owner > panel_index
             correlation, square = lax.psum(
-                (cross(chosen, current), cross(current, current)), ("col", "layer")
+                lax.psum((cross(chosen, current), cross(current, current)), "layer"), "col"
             )
             current = jnp.where(later, current - times(chosen, correlation), current)
             gram_matrix = jnp.where(later, square - cross(correlation, correlation), square)

time: 1730 us -> 1830 us (1.058)
  waiting for transfers between devices: 998 us -> 1100 us
    psum x3 -> x6, waiting for transfers between devices: 183 us -> 282 us  [the longest x3 220 us: orthonormalize(): lax.psum(lax.psum((cross(chosen, current), cross(current, current)), 'lay...]
  transfers between devices with their start and end apart: 12 -> 15, of which waited for: 12 -> 15; matrix products, arithmetic and copies ran while one was open for 0% -> 0% of each run, Pallas kernels for 0% -> 0%
where the time goes in v1:
time: 1830 us; the launch traced here: 1820 us
  waiting for transfers between devices  1100 us (60%)
  other arithmetic  500 us (27%)
  matrix products  137 us (7%)
  local copies, waits for them, and re-layouts  59.8 us (3%)
  between operations  24.6 us (1%)
    psum x4, waiting for transfers between devices, spread(): return lax.psum(jnp.where(mine, x, jnp.zeros_like(x)), axis)  437 us
    another operation x59, other arithmetic, orthonormalize(): factor = jnp.linalg.cholesky(gram_matrix)  319 us
    psum x3, waiting for transfers between devices, orthonormalize(): lax.psum(lax.psum((cross(chosen, current), cross(current, current)), 'lay...  220 us
    another operation x9, other arithmetic, orthonormalize(): jax.scipy.linalg.solve_triangular(factor, current.T, lower=True)  163 us
    all_gather x1, waiting for transfers between devices, shards(): rho_slab = lax.all_gather(rho_part, 'row', axis=1, tiled=True)  152 us
    all_gather x1, waiting for transfers between devices, shards(): own_rows = lax.all_gather(own_slice, 'col', axis=1, tiled=True)  90.3 us
    reduce_scatter x1, waiting for transfers between devices, apply_density(): lax.psum_scatter(cross(rho_slab, basis_block), ('col', 'layer'), scatter_...  69.6 us
    psum x3, waiting for transfers between devices, orthonormalize(): lax.psum((cross(chosen, current), cross(current, current)), 'layer')  62.1 us
  transfers between devices with their start and end apart: 15, of which 15 were waited for; matrix products, arithmetic and copies ran while one was open for 0% of the time, Pallas kernels for 0%

profile of v1, /device:TPU:0, one launch (start us, length us, event | category | flops | bytes accessed | tf_op | source)
XLA Modules:
  0.0 1823.1 jit_solution(13976838146233625954)
XLA Ops:
  9.9 90.3 %all-gather.3.cloned.1.call-done = f32[1024,2048]{1,0:T(8,128)} async-done(((f32[1024,512]{1,0:T(8,128)}), f32[1024,2048]{1,0:T(8,128)}) %all-gather.3.cloned.1.call-update) | async-done | bytes 8388624 | tf_op jit(solution)/shard_map/all_gather | solution.py:59
  108.5 290.9 %all-reduce.19.cloned.1.call-done = f32[1024,2048]{1,0:T(8,128)} async-done(((f32[1024,2048]{1,0:T(8,128)}), f32[1024,2048]{1,0:T(8,128)}) %all-reduce.19.cloned.1.call-update) | async-done | bytes 8388624 | tf_op jit(solution)/shard_map/psum | solution.py:10
  399.4 32.1 %fusion.156 = f32[1024,1024]{1,0:T(8,128)} fusion(f32[1024,2048]{1,0:T(8,128)} %all-reduce.19.cloned.1.call-done, f32[1024,2048]{1,0:T(8,128)} %all-gather.3.cloned.1.call-done), kind=kOutput, calls=%fused_computation.284 | convolution fusion | flops 25769803776 | bytes 20971520 | tf_op jit(solution)/shard_map/dot_general | solution.py:62
  443.0 152.1 %all-gather.5.cloned.1.call-done = f32[512,4096]{1,0:T(8,128)} async-done(((f32[512,1024]{1,0:T(8,128)}), f32[512,4096]{1,0:T(8,128)}) %all-gather.5.cloned.1.call-update) | async-done | bytes 8388624 | tf_op jit(solution)/shard_map/all_gather | solution.py:73
  595.1 17.1 fusion.157
  612.2 69.6 %reduce-scatter.5.cloned.1.call-done = f32[512,512]{0,1:T(8,128)} async-done(((f32[4096,512]{0,1:T(8,128)}), f32[512,512]{0,1:T(8,128)}) %reduce-scatter.5.cloned.1.call-update) | async-done | bytes 1048592 | tf_op jit(solution)/shard_map/reduce_scatter | solution.py:28
  686.6 56.6 %all-reduce.21.cloned.1.call-done = f32[512,512]{0,1:T(8,128)} async-done(((f32[512,512]{0,1:T(8,128)}), f32[512,512]{0,1:T(8,128)}) %all-reduce.21.cloned.1.call-update) | async-done | bytes 1048592 | tf_op jit(solution)/shard_map/psum | solution.py:37
  838.5 39.3 %custom-call.38 = f32[4,128,128]{1,2,0:T(8,128)S(1)} custom-call(f32[4,128,128]{2,1,0:T(8,128)S(1)} %get-tuple-element.33), custom_call_target="InvertDiagBlocksLowerTriangular" | custom-call | tf_op jit(solution)/shard_map/jit(_solve_triangular)/triangular_solve | solution.py:40
  885.2 48.3 %all-reduce.23.cloned.1.call-done = f32[512,512]{0,1:T(8,128)} async-done(((f32[512,512]{0,1:T(8,128)}), f32[512,512]{0,1:T(8,128)}) %all-reduce.23.cloned.1.call-update) | async-done | bytes 1048592 | tf_op jit(solution)/shard_map/psum | solution.py:10
  937.7 20.8 %all-reduce.39.cloned.1.call-done = (f32[512,512]{1,0:T(8,128)}, f32[512,512]{0,1:T(8,128)}) async-done(((f32[512,512]{1,0:T(8,128)}, f32[512,512]{0,1:T(8,128)}), (f32[512,512]{1,0:T(8,128)}, f32[512,512]{0,1:T(8,128)})) %all-reduce.39.cloned.1.call-update) | async-done | bytes 2097168 | tf_op jit(solution)/shard_map/psum | solution.py:46
  958.7 73.5 %all-reduce.33.cloned.1.call-done = (f32[512,512]{1,0:T(8,128)}, f32[512,512]{0,1:T(8,128)}) async-done(((f32[512,512]{1,0:T(8,128)}, f32[512,512]{0,1:T(8,128)}), (f32[512,512]{1,0:T(8,128)}, f32[512,512]{0,1:T(8,128)})) %all-reduce.33.cloned.1.call-update) | async-done | bytes 2097168 | tf_op jit(solution)/shard_map/psum | solution.py:45
  1064.1 12.2 cholesky.553
  1140.2 39.3 %custom-call.42 = f32[4,128,128]{1,2,0:T(8,128)S(1)} custom-call(f32[4,128,128]{2,1,0:T(8,128)S(1)} %get-tuple-element.34), custom_call_target="InvertDiagBlocksLowerTriangular" | custom-call | tf_op jit(solution)/shard_map/jit(_solve_triangular)/triangular_solve | solution.py:40
  1192.7 49.1 %all-reduce.25.cloned.1.call-done = f32[512,512]{0,1:T(8,128)} async-done(((f32[512,512]{0,1:T(8,128)}), f32[512,512]{0,1:T(8,128)}) %all-reduce.25.cloned.1.call-update) | async-done | bytes 1048592 | tf_op jit(solution)/shard_map/psum | solution.py:10
  1245.9 20.8 %all-reduce.37.cloned.1.call-done = (f32[512,512]{1,0:T(8,128)}, f32[512,512]{0,1:T(8,128)}) async-done(((f32[512,512]{1,0:T(8,128)}, f32[512,512]{0,1:T(8,128)}), (f32[512,512]{1,0:T(8,128)}, f32[512,512]{0,1:T(8,128)})) %all-reduce.37.cloned.1.call-update) | async-done | bytes 2097168 | tf_op jit(solution)/shard_map/psum | solution.py:46
  1267.2 73.2 %all-reduce.31.cloned.1.call-done = (f32[512,512]{1,0:T(8,128)}, f32[512,512]{0,1:T(8,128)}) async-done(((f32[512,512]{1,0:T(8,128)}, f32[512,512]{0,1:T(8,128)}), (f32[512,512]{1,0:T(8,128)}, f32[512,512]{0,1:T(8,128)})) %all-reduce.31.cloned.1.call-update) | async-done | bytes 2097168 | tf_op jit(solution)/shard_map/psum | solution.py:45
  1420.5 12.1 cholesky.663
  1448.3 39.3 %custom-call.46 = f32[4,128,128]{1,2,0:T(8,128)S(1)} custom-call(f32[4,128,128]{2,1,0:T(8,128)S(1)} %get-tuple-element.35), custom_call_target="InvertDiagBlocksLowerTriangular" | custom-call | tf_op jit(solution)/shard_map/jit(_solve_triangular)/triangular_solve | solution.py:40
  1500.7 49.1 %all-reduce.27.cloned.1.call-done = f32[512,512]{0,1:T(8,128)} async-done(((f32[512,512]{0,1:T(8,128)}), f32[512,512]{0,1:T(8,128)}) %all-reduce.27.cloned.1.call-update) | async-done | bytes 1048592 | tf_op jit(solution)/shard_map/psum | solution.py:10
  1554.1 20.6 %all-reduce.35.cloned.1.call-done = (f32[512,512]{1,0:T(8,128)}, f32[512,512]{0,1:T(8,128)}) async-done(((f32[512,512]{1,0:T(8,128)}, f32[512,512]{0,1:T(8,128)}), (f32[512,512]{1,0:T(8,128)}, f32[512,512]{0,1:T(8,128)})) %all-reduce.35.cloned.1.call-update) | async-done | bytes 2097168 | tf_op jit(solution)/shard_map/psum | solution.py:46
  1574.8 73.6 %all-reduce.29.cloned.1.call-done = (f32[512,512]{1,0:T(8,128)}, f32[512,512]{0,1:T(8,128)}) async-done(((f32[512,512]{1,0:T(8,128)}, f32[512,512]{0,1:T(8,128)}), (f32[512,512]{1,0:T(8,128)}, f32[512,512]{0,1:T(8,128)})) %all-reduce.29.cloned.1.call-update) | async-done | bytes 2097168 | tf_op jit(solution)/shard_map/psum | solution.py:45
  1733.0 11.9 cholesky.735
  1751.9 13.5 while.11
  1765.4 40.1 %custom-call.50 = f32[4,128,128]{1,2,0:T(8,128)S(1)} custom-call(f32[4,128,128]{2,1,0:T(8,128)} %get-tuple-element.36), custom_call_target="InvertDiagBlocksLowerTriangular" | custom-call | tf_op jit(solution)/shard_map/jit(_solve_triangular)/triangular_solve | solution.py:40
  (262 shorter events, 497.5 us)
Async XLA Ops:
  6.5 588.5 %copy-start = (f32[512,512]{1,0:T(8,128)S(1)}, f32[512,512]{1,0:T(8,128)}, u32[]{:S(2)}) copy-start(f32[512,512]{1,0:T(8,128)} %param.6) | copy-start | bytes 3145732
  6.5 93.6 %all-gather.3.cloned.1.call-start = ((), (), s32[]{:S(2)}) async-start(), calls=%async_computation.2 | async-start | bytes 10485760 | tf_op jit(solution)/shard_map/all_gather | solution.py:59
  9.8 389.6 %all-reduce.19.cloned.1.call-start = ((), (), s32[]{:S(2)}) async-start(), calls=%async_computation.3 | async-start | bytes 16777216 | tf_op jit(solution)/shard_map/psum | solution.py:10
  108.4 334.3 %reduce-scatter.3.cloned.1.call-start = ((), (), s32[]{:S(2)}) async-start(), calls=%async_computation.4 | async-start | bytes 6291456 | tf_op jit(solution)/shard_map/reduce_scatter | solution.py:61
  431.5 163.5 %all-gather.5.cloned.1.call-start = ((), (), s32[]{:S(2)}) async-start(), calls=%async_computation.5 | async-start | bytes 10485760 | tf_op jit(solution)/shard_map/all_gather | solution.py:73
  442.7 239.1 %reduce-scatter.5.cloned.1.call-start = ((), (), s32[]{:S(2)}) async-start(), calls=%async_computation.6 | async-start | bytes 9437184 | tf_op jit(solution)/shard_map/reduce_scatter | solution.py:28
  612.2 131.0 %all-reduce.21.cloned.1.call-start = ((), (), s32[]{:S(2)}) async-start(), calls=%async_computation.7 | async-start | bytes 2097152 | tf_op jit(solution)/shard_map/psum | solution.py:37
  681.8 196.0 %copy-start.2 = (f32[512,512]{0,1:T(8,128)S(1)}, f32[512,512]{0,1:T(8,128)}, u32[]{:S(2)}) copy-start(f32[512,512]{0,1:T(8,128)} %reduce-scatter.5.cloned.1.call-done) | copy-start | bytes 3145732
  686.3 247.2 %all-reduce.23.cloned.1.call-start = ((), (), s32[]{:S(2)}) async-start(), calls=%async_computation.8 | async-start | bytes 2097152 | tf_op jit(solution)/shard_map/psum | solution.py:10
  882.2 76.2 %all-reduce.39.cloned.1.call-start = ((), (), s32[]{:S(2)}) async-start(), calls=%async_computation.16 | async-start | bytes 4194304 | tf_op jit(solution)/shard_map/psum | solution.py:46
  937.6 94.6 %all-reduce.33.cloned.1.call-start = ((), (), s32[]{:S(2)}) async-start(), calls=%async_computation.13 | async-start | bytes 4194304 | tf_op jit(solution)/shard_map/psum | solution.py:45
  958.4 283.3 %all-reduce.25.cloned.1.call-start = ((), (), s32[]{:S(2)}) async-start(), calls=%async_computation.9 | async-start | bytes 2097152 | tf_op jit(solution)/shard_map/psum | solution.py:10
  1032.2 147.3 %copy-start.4 = (f32[512,512]{1,0:T(8,128)S(1)}, f32[512,512]{1,0:T(8,128)}, u32[]{:S(2)}) copy-start(f32[512,512]{1,0:T(8,128)} %get-tuple-element.73) | copy-start | bytes 3145732
  1038.9 1.0 copy-start.6
  1189.7 76.9 %all-reduce.37.cloned.1.call-start = ((), (), s32[]{:S(2)}) async-start(), calls=%async_computation.15 | async-start | bytes 4194304 | tf_op jit(solution)/shard_map/psum | solution.py:46
  1245.9 94.5 %all-reduce.31.cloned.1.call-start = ((), (), s32[]{:S(2)}) async-start(), calls=%async_computation.12 | async-start | bytes 4194304 | tf_op jit(solution)/shard_map/psum | solution.py:45
  1266.7 283.1 %all-reduce.27.cloned.1.call-start = ((), (), s32[]{:S(2)}) async-start(), calls=%async_computation.10 | async-start | bytes 2097152 | tf_op jit(solution)/shard_map/psum | solution.py:10
  1340.3 147.3 %copy-start.5 = (f32[512,512]{1,0:T(8,128)S(1)}, f32[512,512]{1,0:T(8,128)}, u32[]{:S(2)}) copy-start(f32[512,512]{1,0:T(8,128)} %get-tuple-element.71) | copy-start | bytes 3145732
  1347.0 1.0 copy-start.7
  1497.8 76.9 %all-reduce.35.cloned.1.call-start = ((), (), s32[]{:S(2)}) async-start(), calls=%async_computation.14 | async-start | bytes 4194304 | tf_op jit(solution)/shard_map/psum | solution.py:46
  1553.9 94.4 %all-reduce.29.cloned.1.call-start = ((), (), s32[]{:S(2)}) async-start(), calls=%async_computation.11 | async-start | bytes 4194304 | tf_op jit(solution)/shard_map/psum | solution.py:45
  1648.4 157.2 %copy-start.3 = (f32[512,512]{1,0:T(8,128)S(1)}, f32[512,512]{1,0:T(8,128)}, u32[]{:S(2)}) copy-start(f32[512,512]{1,0:T(8,128)} %get-tuple-element.69) | copy-start | bytes 3145732
  1655.1 1.0 copy-start.8
  1748.7 67.4 %copy-start.1 = (f32[512,512]{1,0:T(8,128)S(1)}, f32[512,512]{1,0:T(8,128)}, u32[]{:S(2)}) copy-start(f32[512,512]{1,0:T(8,128)} %param.6) | copy-start | bytes 3145732
Sparse Core Ops, SparseCore 0:
  9.9 90.1 all-gather.2
  108.5 290.8 all-reduce.18
  431.7 10.9 reduce-scatter.2
  444.1 150.8 all-gather.4
  612.3 69.4 reduce-scatter.4
  686.5 56.7 all-reduce.20
  882.4 51.1 all-reduce.22
  937.7 20.6 all-reduce.38
  961.5 70.6 all-reduce.32
  1189.9 51.8 all-reduce.24
  1246.0 20.6 all-reduce.36
  1269.6 70.6 all-reduce.30
  1497.9 51.8 all-reduce.26
  1554.0 20.6 all-reduce.34
  1577.7 70.6 all-reduce.28
